TPU v7x, 128 devices: a whole 4x4x4 slice. The times are simulated.
128 devices in a mesh: section: 2 (over x_hi), dp: 16 (over z, y), mp: 4 (over x_lo, core).
Axes of the slice: x: 4 (x_hi: 2, x_lo: 2; x = x_hi * 2 + x_lo), y: 4, z: 4, core: 2. Of those that a mesh axis runs over, the one named last changes fastest.
Arguments:
- text_feats: bfloat16 [16384, 512], P('dp'), may hold values from -48 to 48
- image_feats: bfloat16 [16384, 512], P(('dp', 'mp')), may hold values from -48 to 48
- logit_scale: float32 [1], replicated, may hold values from 10 to 320
- layer_inputs: bfloat16 [2, 16384, 512], P('section', 'dp'), may hold values from -6 to 6
- w_in: bfloat16 [2, 512, 2048], P('section', None, 'mp'), may hold values from -0.25 to 0.25
- w_out: bfloat16 [2, 2048, 512], P('section', 'mp'), may hold values from -0.125 to 0.125
Outputs:
- image_grad: bfloat16 [16384, 512], P(('dp', 'mp'))
- input_grad: bfloat16 [16384, 512], P('dp', 'section')
- w_in_grad: float32 [2, 512, 2048], P('section', 'dp', 'mp')
- w_out_grad_t: float32 [2, 512, 2048], P('section', 'dp', 'mp')
All inputs are finite; a program needn't handle non-finite values.
Results may differ from a plain program's by a relative error of at most 0.017.
Values may be sent and summed in bfloat16 or wider, within the bound.
No kernel may reach another device: no remote copies, remote signals or barrier semaphores. Data moves between devices by JAX's collectives and lax.ppermute only.
A program may use at most 128 MiB of HBM per device.

v0:
```python
import jax
import jax.numpy as jnp
from jax import lax
from jax.sharding import PartitionSpec as P

MICRO = 4


def from_everyone(array, axis):
    copies = jnp.broadcast_to(array, (lax.axis_size(axis), *array.shape))
    return lax.all_to_all(copies, axis, split_axis=0, concat_axis=0, tiled=True)


def collected_together(array, axis):
    leaves = jax.tree.leaves(array)
    sequence = sorted(range(len(leaves)), key=lambda k: -leaves[k].size)
    width = (1, *leaves[sequence[0]].shape)[-1]
    lines = [
        jnp.pad(leaves[k].reshape(-1), (0, -leaves[k].size % width)).reshape(-1, width)
        for k in sequence
    ]
    both, at, found = (from_everyone(jnp.concatenate(lines), axis), 0, {})
    for k, line in zip(sequence, lines):
        slab = both[:, at : at + len(line)].reshape(len(both), -1)
        found[k] = slab[:, : leaves[k].size].reshape(-1, *leaves[k].shape)
        at += len(line)
    numbers = iter(range(len(leaves)))
    return jax.tree.map(lambda _: found[next(numbers)], array)


def combined_pairwise(pieces, combine):
    while len(jax.tree.leaves(pieces)[0]) > 1:
        pieces = jax.vmap(combine)(
            *(jax.tree.map(lambda part: part[side::2], pieces) for side in (0, 1))
        )
    return jax.tree.map(lambda part: part[0], pieces)


def joined_all(array, axis, combine):
    pieces = collected_together(array, axis)
    return combined_pairwise(pieces, combine)


def of_everyone(array, axis):
    return from_everyone(array, axis).astype(jnp.float32).sum(axis=0)


def shifted(block, axis, distance):
    devices = range(lax.axis_size(axis))
    route = [(i - distance, i) for i in devices if i - distance in devices]
    return lax.ppermute(block, axis, route)


def picked(array, axis, root):
    return lax.dynamic_index_in_dim(lax.all_gather(array, axis), root, 0, keepdims=False)


def in_one_piece(arrays, axis, dim, along):
    both = jnp.concatenate(arrays, axis=along)
    result, at, done = (lax.psum_scatter(both, axis, scatter_dimension=dim, tiled=True), 0, [])
    for a in arrays:
        done.append(lax.slice_in_dim(result, at, at + a.shape[along], axis=along))
        at += a.shape[along]
    return tuple(done)


def unit_rows(values):
    wide = values.astype(jnp.float32)
    length = jnp.sqrt(jnp.sum(wide * wide, axis=1, keepdims=True) + 1.0)
    return (wide / length, length)


def unit_backward(unit, length, grad_unit):
    return (grad_unit - unit * jnp.sum(unit * grad_unit, axis=1, keepdims=True)) / length


def quick_gelu(values):
    return values * jax.nn.sigmoid(1.702 * values)


def quick_slope(values):
    sigm = jax.nn.sigmoid(1.702 * values)
    return sigm + 1.702 * values * sigm * (1.0 - sigm)


def joined_softmax(left_pair, right_pair):
    peak_value = jnp.maximum(left_pair[0], right_pair[0])
    total = left_pair[1] * jnp.exp(left_pair[0] - peak_value) + right_pair[1] * jnp.exp(
        right_pair[0] - peak_value
    )
    return (peak_value, total)


def contract_rows(left_side, right_side):
    return lax.dot_general(
        left_side, right_side, (((0,), (0,)), ((), ())), preferred_element_type=jnp.float32
    )


def contract_cols(left_side, right_side):
    return lax.dot_general(
        left_side, right_side, (((1,), (1,)), ((), ())), preferred_element_type=jnp.float32
    )


def body(text_feats, image_feats, logit_scale, layer_inputs, w_in, w_out):
    logit_mult = logit_scale[0]
    mp_count = lax.axis_size("mp")
    segment_count = lax.axis_size("section")
    dp_index = lax.axis_index("dp")
    mp_index = lax.axis_index("mp")
    segment_index = lax.axis_index("section")
    row_count = text_feats.shape[0]
    own_rows = image_feats.shape[0]
    text_unit, text_length = unit_rows(text_feats)
    image_unit, image_length = unit_rows(image_feats)
    text_low = text_unit.astype(jnp.bfloat16)
    image_low = image_unit.astype(jnp.bfloat16)
    columns = lax.all_gather(image_low, "dp", axis=0, tiled=True)
    column_total_count = columns.shape[0]
    scores = logit_mult * contract_cols(text_low, columns)
    text_ids = dp_index * row_count + jnp.arange(row_count, dtype=jnp.int32)
    column_pos = jnp.arange(column_total_count, dtype=jnp.int32)
    image_ids = (column_pos // own_rows * mp_count + mp_index) * own_rows + column_pos % own_rows
    positive = (text_ids[:, None] == image_ids[None, :]).astype(jnp.float32)
    local_rpeak = jnp.max(scores, axis=1)
    local_cpeak = jnp.max(scores, axis=0)
    row_peak, row_total = joined_all(
        (local_rpeak, jnp.sum(jnp.exp(scores - local_rpeak[:, None]), axis=1)), "mp", joined_softmax
    )
    column_local = jnp.sum(jnp.exp(scores - local_cpeak[None, :]), axis=0)
    column_peak, column_total = joined_all((local_cpeak, column_local), "dp", joined_softmax)
    row_prob = jnp.exp(scores - row_peak[:, None]) / row_total[:, None]
    column_prob = jnp.exp(scores - column_peak[None, :]) / column_total[None, :]
    score_grad = (0.5 * (row_prob + column_prob) - positive).astype(jnp.bfloat16)
    text_share = logit_mult * jnp.dot(score_grad, columns, preferred_element_type=jnp.float32)
    text_unit_grad = of_everyone(text_share.astype(jnp.bfloat16), "mp").astype(jnp.float32)
    top_grad = unit_backward(text_unit, text_length, text_unit_grad).astype(jnp.bfloat16)
    image_unit_grad = lax.psum_scatter(
        (logit_mult * contract_rows(score_grad, text_low)).astype(jnp.bfloat16),
        "dp",
        scatter_dimension=0,
        tiled=True,
    ).astype(jnp.float32)
    image_grad = unit_backward(image_unit, image_length, image_unit_grad).astype(jnp.bfloat16)
    segment_inputs = layer_inputs[0]
    w_first = w_in[0]
    w_second = w_out[0]
    step_rows = row_count // MICRO
    last_segment = segment_count - 1
    time_steps = MICRO + segment_count - 1
    is_last = segment_index == last_segment
    is_first = segment_index == 0
    incoming = jnp.zeros((step_rows, segment_inputs.shape[1]), jnp.bfloat16)
    grad_first = jnp.zeros(w_first.shape, jnp.float32)
    grad_second = jnp.zeros(w_first.shape, jnp.float32)
    finished = jnp.zeros((row_count, segment_inputs.shape[1]), jnp.bfloat16)
    for time_step in range(time_steps):
        micro_slot = time_step - last_segment + segment_index
        active = jnp.logical_and(micro_slot >= 0, micro_slot < MICRO)
        row_start = jnp.clip(micro_slot, 0, MICRO - 1) * step_rows
        top_start = min(time_step, MICRO - 1) * step_rows
        top_piece = top_grad[top_start : top_start + step_rows]
        grad_now = jnp.where(is_last, top_piece, incoming)
        inputs_now = lax.dynamic_slice_in_dim(segment_inputs, row_start, step_rows, 0)
        pre_act = jnp.dot(inputs_now, w_first, preferred_element_type=jnp.float32)
        activation = quick_gelu(pre_act).astype(jnp.bfloat16)
        back_grad = contract_cols(grad_now, w_second)
        pre_grad = (back_grad * quick_slope(pre_act)).astype(jnp.bfloat16)
        unit_share = contract_cols(pre_grad, w_first)
        summed = of_everyone(unit_share.astype(jnp.bfloat16), "mp").astype(jnp.float32)
        grad_prev = (grad_now.astype(jnp.float32) + summed).astype(jnp.bfloat16)
        weight = active.astype(jnp.float32)
        grad_first = grad_first + weight * contract_rows(inputs_now, pre_grad)
        grad_second = grad_second + weight * contract_rows(grad_now, activation)
        updated = lax.dynamic_update_slice_in_dim(finished, grad_prev, row_start, 0)
        finished = jnp.where(jnp.logical_and(active, is_first), updated, finished)
        if time_step + 1 < time_steps:
            incoming = shifted(grad_prev, "section", -1)
    whole_grad = picked(finished, "section", 0)
    feature_width = whole_grad.shape[1] // segment_count
    feature_start = segment_index * feature_width
    input_grad = lax.dynamic_slice_in_dim(whole_grad, feature_start, feature_width, 1)
    first_sum, second_sum = tuple(
        (
            part.astype(jnp.float32)
            for part in in_one_piece(
                (grad_first.astype(jnp.bfloat16), grad_second.astype(jnp.bfloat16)), "dp", 0, 1
            )
        )
    )
    return (image_grad, input_grad, first_sum[None], second_sum[None])


def solution(mesh):
    placed = (
        P("dp", None),
        P(("dp", "mp"), None),
        P(),
        P("section", "dp", None),
        P("section", None, "mp"),
        P("section", "mp", None),
    )
    return jax.shard_map(
        body,
        mesh=mesh,
        in_specs=placed,
        out_specs=(
            P(("dp", "mp"), None),
            P("dp", "section"),
            P("section", "dp", "mp"),
            P("section", "dp", "mp"),
        ),
        check_vma=False,
    )
```

profile of v0, /device:TPU:1, one launch (start us, length us, event | category | flops | bytes accessed | tf_op | source)
XLA Modules:
  0.0 463.0 jit_solution(3558980149796986611)
XLA Ops:
  7.2 1.2 fusion.16
  8.4 1.8 fusion.113
  10.9 1.5 fusion
  12.4 52.9 %all-gather.3.cloned.1.call-done = bf16[4096,512]{1,0:T(8,128)(2,1)} async-done(((bf16[256,512]{1,0:T(8,128)(2,1)}), bf16[4096,512]{1,0:T(8,128)(2,1)}) %all-gather.3.cloned.1.call-update) | async-done | bytes 4194320 | tf_op jit(solution)/shard_map/all_gather | solution.py:119
  65.3 6.8 %multiply_reduce_fusion.1 = (f32[1024]{0:T(1024)S(1)}, f32[1024,4096]{1,0:T(8,128)S(1)}) fusion(f32[]{:T(128)} %bitcast.111, bf16[4096,512]{1,0:T(8,128)(2,1)} %all-gather.3.cloned.1.call-done, f32[1024]{0:T(1024)S(1)} %add_sqrt_fusion, bf16[1024,512]{1,0:T(8,128)(2,1)} %param.6), kind=kOutput, calls=%fused_computation.4 | convolution fusion | flops 4304927744 | bytes 22028292 | tf_op jit(solution)/shard_map/dot_general | solution.py:101
  72.1 4.3 exponential_reduce_fusion.1
  76.5 1.4 copy-done.1
  78.5 4.1 all-to-all-start
  82.6 8.5 %exponential_reduce_fusion = f32[4096]{0:T(1024)S(1)} fusion(f32[1024,4096]{1,0:T(8,128)} %copy-done.1, f32[4096]{0:T(1024)S(1)} %get-tuple-element.17, f32[]{:T(128)} %bitcast.115), kind=kLoop, calls=%fused_computation.1 | loop fusion | flops 12578816 | bytes 16809988 | tf_op jit(solution)/shard_map/reduce_sum | solution.py:131
  92.1 5.0 %all-to-all-start.1 = ((f32[16,2,4096]{2,1,0:T(2,128)}), f32[16,2,4096]{2,1,0:T(2,128)S(1)}, u32[]{:S(2)}, u32[]{:S(2)}) async-start(f32[16,2,4096]{2,1,0:T(2,128)} %broadcast_in_dim.51), calls=%async_computation.1 | async-start | bytes 1048576 | tf_op jit(solution)/shard_map/all_to_all | solution.py:11
  97.4 10.8 %all-to-all-done.1 = f32[16,2,4096]{2,1,0:T(2,128)S(1)} async-done(((f32[16,2,4096]{2,1,0:T(2,128)}), f32[16,2,4096]{2,1,0:T(2,128)S(1)}, u32[]{:S(2)}, u32[]{:S(2)}) %all-to-all-start.1) | async-done | bytes 524320 | tf_op jit(solution)/shard_map/all_to_all | solution.py:11
  110.7 11.4 %subtract_convert_fusion = bf16[1024,4096]{1,0:T(8,128)(2,1)S(1)} fusion(f32[1024,4096]{1,0:T(8,128)} %copy-done.1, s32[4096]{0:T(1024)S(1)} %fusion.87, f32[4096]{0:T(1024)S(1)} %bitcast.117, f32[4096]{0:T(1024)S(1)} %bitcast.118, f32[1024]{0:T(1024)S(1)} %bitcast.120, f32[1024]{0:T(1024)S(1)} %bitcast.121, f32[]{:T(128)} %bitcast.114, s32[1024]{0:T(1024)S(1)} %iota_add_fusion), kind=kLoop, calls=%fused_computation | loop fusion | flops 46137344 | bytes 25227268 | tf_op jit(solution)/shard_map/convert_element_type | solution.py:135
  122.1 3.3 copy-done.4
  125.4 4.5 multiply_convert_fusion.1
  129.9 2.3 broadcast_in_dim.53
  132.1 6.5 %all-to-all-start.2 = ((bf16[4,1024,512]{2,1,0:T(8,128)(2,1)}), bf16[4,1024,512]{2,1,0:T(8,128)(2,1)}, u32[]{:S(2)}, u32[]{:S(2)}) async-start(bf16[4,1024,512]{2,1,0:T(8,128)(2,1)} %broadcast_in_dim.53), calls=%async_computation.3 | async-start | bytes 8388608 | tf_op jit(solution)/shard_map/all_to_all | solution.py:11
  139.0 47.0 %all-to-all-done.2 = bf16[4,1024,512]{2,1,0:T(8,128)(2,1)} async-done(((bf16[4,1024,512]{2,1,0:T(8,128)(2,1)}), bf16[4,1024,512]{2,1,0:T(8,128)(2,1)}, u32[]{:S(2)}, u32[]{:S(2)}) %all-to-all-start.2) | async-done | bytes 4194336 | tf_op jit(solution)/shard_map/all_to_all | solution.py:11
  185.9 3.2 convert_reduce_fusion
  193.7 5.2 %all-to-all-start.3 = ((bf16[4,256,512]{2,1,0:T(8,128)(2,1)}), bf16[4,256,512]{2,1,0:T(8,128)(2,1)}, u32[]{:S(2)}, u32[]{:S(2)}) async-start(bf16[4,256,512]{2,1,0:T(8,128)(2,1)} %broadcast_in_dim.55), calls=%async_computation.4 | async-start | bytes 2097152 | tf_op jit(solution)/shard_map/all_to_all | solution.py:11
  199.2 13.3 %all-to-all-done.3 = bf16[4,256,512]{2,1,0:T(8,128)(2,1)} async-done(((bf16[4,256,512]{2,1,0:T(8,128)(2,1)}), bf16[4,256,512]{2,1,0:T(8,128)(2,1)}, u32[]{:S(2)}, u32[]{:S(2)}) %all-to-all-start.3) | async-done | bytes 1048608 | tf_op jit(solution)/shard_map/all_to_all | solution.py:11
  212.4 1.4 convert_reduce_fusion.5
  214.9 1.8 select_dynamic-update-slice_fusion.3
  216.7 1.5 collective-permute-start
  218.2 9.9 %multiply_convert_fusion = bf16[4096,512]{1,0:T(8,128)(2,1)} fusion(bf16[1024,4096]{1,0:T(8,128)(2,1)} %copy-done.4, f32[]{:T(128)} %bitcast.110, bf16[1024,512]{1,0:T(8,128)(2,1)S(1)} %copy-done.3, f32[1024]{0:T(1024)S(1)} %add_sqrt_fusion), kind=kOutput, calls=%fused_computation.6 | convolution fusion | flops 4300734464 | bytes 13635588 | tf_op jit(solution)/shard_map/dot_general | solution.py:95
  229.3 1.5 fusion.12
  232.9 5.2 %all-to-all-start.4 = ((bf16[4,256,512]{2,1,0:T(8,128)(2,1)}), bf16[4,256,512]{2,1,0:T(8,128)(2,1)}, u32[]{:S(2)}, u32[]{:S(2)}) async-start(bf16[4,256,512]{2,1,0:T(8,128)(2,1)} %broadcast_in_dim.56), calls=%async_computation.5 | async-start | bytes 2097152 | tf_op jit(solution)/shard_map/all_to_all | solution.py:11
  238.1 13.6 %all-to-all-done.4 = bf16[4,256,512]{2,1,0:T(8,128)(2,1)} async-done(((bf16[4,256,512]{2,1,0:T(8,128)(2,1)}), bf16[4,256,512]{2,1,0:T(8,128)(2,1)}, u32[]{:S(2)}, u32[]{:S(2)}) %all-to-all-start.4) | async-done | bytes 1048608 | tf_op jit(solution)/shard_map/all_to_all | solution.py:11
  251.7 1.4 convert_reduce_fusion.4
  253.1 1.9 select_dynamic-update-slice_fusion.2
  255.0 1.3 collective-permute-start.1
  256.6 9.9 %collective-permute-done.1 = bf16[256,512]{1,0:T(8,128)(2,1)} collective-permute-done((bf16[256,512]{1,0:T(8,128)(2,1)}, bf16[256,512]{1,0:T(8,128)(2,1)}, u32[]{:S(2)}, u32[]{:S(2)}) %collective-permute-start.1) | collective-permute-done | bytes 262176 | tf_op jit(solution)/shard_map/ppermute | solution.py:51
  267.5 1.5 fusion.13
  271.1 5.7 %all-to-all-start.5 = ((bf16[4,256,512]{2,1,0:T(8,128)(2,1)}), bf16[4,256,512]{2,1,0:T(8,128)(2,1)}, u32[]{:S(2)}, u32[]{:S(2)}) async-start(bf16[4,256,512]{2,1,0:T(8,128)(2,1)} %broadcast_in_dim.57), calls=%async_computation.6 | async-start | bytes 2097152 | tf_op jit(solution)/shard_map/all_to_all | solution.py:11
  279.0 2.3 convolution_multiply_fusion.9
  281.3 2.4 convolution_multiply_fusion.4
  283.7 6.6 %all-to-all-done.5 = bf16[4,256,512]{2,1,0:T(8,128)(2,1)} async-done(((bf16[4,256,512]{2,1,0:T(8,128)(2,1)}), bf16[4,256,512]{2,1,0:T(8,128)(2,1)}, u32[]{:S(2)}, u32[]{:S(2)}) %all-to-all-start.5) | async-done | bytes 1048608 | tf_op jit(solution)/shard_map/all_to_all | solution.py:11
  290.3 1.4 convert_reduce_fusion.3
  291.8 1.8 select_dynamic-update-slice_fusion.1
  293.6 1.3 collective-permute-start.2
  294.9 2.8 fusion.2
  297.7 6.2 %collective-permute-done.2 = bf16[256,512]{1,0:T(8,128)(2,1)S(1)} collective-permute-done((bf16[256,512]{1,0:T(8,128)(2,1)S(1)}, bf16[256,512]{1,0:T(8,128)(2,1)S(1)}, u32[]{:S(2)}, u32[]{:S(2)}) %collective-permute-start.2) | collective-permute-done | bytes 262176 | tf_op jit(solution)/shard_map/ppermute | solution.py:51
  304.6 1.6 fusion.14
  308.4 6.0 %all-to-all-start.6 = ((bf16[4,256,512]{2,1,0:T(8,128)(2,1)}), bf16[4,256,512]{2,1,0:T(8,128)(2,1)}, u32[]{:S(2)}, u32[]{:S(2)}) async-start(bf16[4,256,512]{2,1,0:T(8,128)(2,1)} %broadcast_in_dim.58), calls=%async_computation.7 | async-start | bytes 2097152 | tf_op jit(solution)/shard_map/all_to_all | solution.py:11
  314.3 1.6 fusion.6
  316.0 1.3 fusion.5
  317.3 2.3 fusion.4
  319.6 8.3 %all-to-all-done.6 = bf16[4,256,512]{2,1,0:T(8,128)(2,1)} async-done(((bf16[4,256,512]{2,1,0:T(8,128)(2,1)}), bf16[4,256,512]{2,1,0:T(8,128)(2,1)}, u32[]{:S(2)}, u32[]{:S(2)}) %all-to-all-start.6) | async-done | bytes 1048608 | tf_op jit(solution)/shard_map/all_to_all | solution.py:11
  327.9 1.6 convert_reduce_fusion.2
  329.5 1.8 select_dynamic-update-slice_fusion
  331.3 1.3 collective-permute-start.3
  332.6 1.5 convolution_multiply_fusion.1
  334.1 7.5 %collective-permute-done.3 = bf16[256,512]{1,0:T(8,128)(2,1)S(1)} collective-permute-done((bf16[256,512]{1,0:T(8,128)(2,1)S(1)}, bf16[256,512]{1,0:T(8,128)(2,1)S(1)}, u32[]{:S(2)}, u32[]{:S(2)}) %collective-permute-start.3) | collective-permute-done | bytes 262176 | tf_op jit(solution)/shard_map/ppermute | solution.py:51
  341.7 1.7 fusion.15
  344.7 1.3 copy.22
  346.0 1.3 convolution_convert_fusion
  348.5 5.3 %all-to-all-start.7 = ((bf16[4,256,512]{2,1,0:T(8,128)(2,1)}), bf16[4,256,512]{2,1,0:T(8,128)(2,1)S(1)}, u32[]{:S(2)}, u32[]{:S(2)}) async-start(bf16[4,256,512]{2,1,0:T(8,128)(2,1)} %broadcast_in_dim.59), calls=%async_computation.8 | async-start | bytes 2097152 | tf_op jit(solution)/shard_map/all_to_all | solution.py:11
  353.8 2.3 copy.38
  356.0 11.3 %all-to-all-done.7 = bf16[4,256,512]{2,1,0:T(8,128)(2,1)S(1)} async-done(((bf16[4,256,512]{2,1,0:T(8,128)(2,1)}), bf16[4,256,512]{2,1,0:T(8,128)(2,1)S(1)}, u32[]{:S(2)}, u32[]{:S(2)}) %all-to-all-start.7) | async-done | bytes 1048608 | tf_op jit(solution)/shard_map/all_to_all | solution.py:11
  367.5 1.8 fusion.45
  369.3 1.2 fusion.17
  370.5 1.9 fusion.19
  372.4 42.6 %reduce-scatter.7.cloned.1.call-done = bf16[32,1024]{1,0:T(8,128)(2,1)} async-done(((bf16[512,1024]{1,0:T(8,128)(2,1)}), bf16[32,1024]{1,0:T(8,128)(2,1)}) %reduce-scatter.7.cloned.1.call-update) | async-done | bytes 65552
  417.5 36.8 %all-gather.5.cloned.1.call-done = bf16[2,1024,512]{2,1,0:T(8,128)(2,1)} async-done(((bf16[1,1024,512]{2,1,0:T(8,128)(2,1)}), bf16[2,1024,512]{2,1,0:T(8,128)(2,1)}) %all-gather.5.cloned.1.call-update) | async-done | bytes 2097168 | tf_op jit(solution)/shard_map/all_gather | solution.py:55
  454.3 1.3 dynamic_slice.47
  (126 shorter events, 28.2 us)
Async XLA Ops:
  7.2 131.5 %copy-start = (bf16[1,1024,512]{2,1,0:T(8,128)(2,1)S(1)}, bf16[1,1024,512]{2,1,0:T(8,128)(2,1)}, u32[]{:S(2)}) copy-start(bf16[1,1024,512]{2,1,0:T(8,128)(2,1)} %param.9) | copy-start | bytes 3145732
  7.2 58.1 %all-gather.3.cloned.1.call-start = ((), (), s32[]{:S(2)}) async-start(), calls=%async_computation.10 | async-start | bytes 4456448 | tf_op jit(solution)/shard_map/all_gather | solution.py:119
  72.1 5.7 %copy-start.1 = (f32[1024,4096]{1,0:T(8,128)}, f32[1024,4096]{1,0:T(8,128)S(1)}, u32[]{:S(2)}) copy-start(f32[1024,4096]{1,0:T(8,128)S(1)} %get-tuple-element.45) | copy-start | bytes 50331652
  78.5 12.6 %all-to-all-start = ((f32[4,2,1024]{2,1,0:T(2,128)}), f32[4,2,1024]{2,1,0:T(2,128)S(1)}, u32[]{:S(2)}, u32[]{:S(2)}) async-start(f32[4,2,1024]{2,1,0:T(2,128)} %broadcast_in_dim.50), calls=%async_computation | async-start | bytes 65536 | tf_op jit(solution)/shard_map/all_to_all | solution.py:11
  92.1 16.0 %all-to-all-start.1 = ((f32[16,2,4096]{2,1,0:T(2,128)}), f32[16,2,4096]{2,1,0:T(2,128)S(1)}, u32[]{:S(2)}, u32[]{:S(2)}) async-start(f32[16,2,4096]{2,1,0:T(2,128)} %broadcast_in_dim.51), calls=%async_computation.1 | async-start | bytes 1048576 | tf_op jit(solution)/shard_map/all_to_all | solution.py:11
  110.7 14.7 %copy-start.22 = (bf16[4096,512]{1,0:T(8,128)(2,1)S(1)}, bf16[4096,512]{1,0:T(8,128)(2,1)}, u32[]{:S(2)}) copy-start(bf16[4096,512]{1,0:T(8,128)(2,1)} %all-gather.3.cloned.1.call-done) | copy-start | bytes 12582916
  122.1 3.3 copy-start.4
  129.9 8.8 %copy-start.2 = (bf16[1,512,512]{2,1,0:T(8,128)(2,1)S(1)}, bf16[1,512,512]{2,1,0:T(8,128)(2,1)}, u32[]{:S(2)}) copy-start(bf16[1,512,512]{2,1,0:T(8,128)(2,1)} %param.10) | copy-start | bytes 1572868
  132.1 57.0 %copy-start.3 = (bf16[1024,512]{1,0:T(8,128)(2,1)S(1)}, bf16[1024,512]{1,0:T(8,128)(2,1)}, u32[]{:S(2)}) copy-start(bf16[1024,512]{1,0:T(8,128)(2,1)} %param.6) | copy-start | bytes 3145732
  132.1 53.8 %all-to-all-start.2 = ((bf16[4,1024,512]{2,1,0:T(8,128)(2,1)}), bf16[4,1024,512]{2,1,0:T(8,128)(2,1)}, u32[]{:S(2)}, u32[]{:S(2)}) async-start(bf16[4,1024,512]{2,1,0:T(8,128)(2,1)} %broadcast_in_dim.53), calls=%async_computation.3 | async-start | bytes 8388608 | tf_op jit(solution)/shard_map/all_to_all | solution.py:11
  139.0 52.6 %copy-start.19 = (f32[256,512]{1,0:T(8,128)}, f32[256,512]{1,0:T(8,128)S(1)}, u32[]{:S(2)}) copy-start(f32[256,512]{1,0:T(8,128)S(1)} %fusion.33) | copy-start | bytes 1572868
  185.9 5.2 %copy-start.23 = (bf16[1,512,512]{2,1,0:T(8,128)(2,1)S(1)}, bf16[1,512,512]{2,1,0:T(8,128)(2,1)}, u32[]{:S(2)}) copy-start(bf16[1,512,512]{2,1,0:T(8,128)(2,1)} %param.11) | copy-start | bytes 1572868
  190.1 1.0 copy-start.5
  191.6 0.7 copy-start.13
  193.7 18.8 %all-to-all-start.3 = ((bf16[4,256,512]{2,1,0:T(8,128)(2,1)}), bf16[4,256,512]{2,1,0:T(8,128)(2,1)}, u32[]{:S(2)}, u32[]{:S(2)}) async-start(bf16[4,256,512]{2,1,0:T(8,128)(2,1)} %broadcast_in_dim.55), calls=%async_computation.4 | async-start | bytes 2097152 | tf_op jit(solution)/shard_map/all_to_all | solution.py:11
  198.9 170.4 %reduce-scatter.5.cloned.1.call-start = ((), (), s32[]{:S(2)}) async-start(), calls=%async_computation.11 | async-start | bytes 4456448 | tf_op jit(solution)/shard_map/reduce_scatter | solution.py:139
  199.2 30.1 %copy-start.20 = (f32[256,512]{1,0:T(8,128)}, f32[256,512]{1,0:T(8,128)S(1)}, u32[]{:S(2)}) copy-start(f32[256,512]{1,0:T(8,128)S(1)} %fusion.30) | copy-start | bytes 1572868
  216.7 11.4 %collective-permute-start = (bf16[256,512]{1,0:T(8,128)(2,1)S(1)}, bf16[256,512]{1,0:T(8,128)(2,1)}, u32[]{:S(2)}, u32[]{:S(2)}) collective-permute-start(bf16[256,512]{1,0:T(8,128)(2,1)S(1)} %get-tuple-element.25), channel_id=1, source_target_pairs={{64,0},{65,1},{66,2},{67,3},{68,4},{69,5},{70,6},{71,7},{72,8},{73... | collective-permute-start | bytes 786440 | tf_op jit(solution)/shard_map/ppermute | solution.py:51
  228.1 38.4 %copy-start.6 = (bf16[1024,512]{1,0:T(8,128)(2,1)S(1)}, bf16[1024,512]{1,0:T(8,128)(2,1)}, u32[]{:S(2)}) copy-start(bf16[1024,512]{1,0:T(8,128)(2,1)} %copy-done.5) | copy-start | bytes 3145732
  229.3 27.3 %copy-start.14 = (bf16[256,512]{1,0:T(8,128)(2,1)}, bf16[256,512]{1,0:T(8,128)(2,1)S(1)}, u32[]{:S(2)}) copy-start(bf16[256,512]{1,0:T(8,128)(2,1)S(1)} %slice_select_fusion.1) | copy-start | bytes 786436
  230.8 0.7 copy-start.10
  232.9 18.7 %all-to-all-start.4 = ((bf16[4,256,512]{2,1,0:T(8,128)(2,1)}), bf16[4,256,512]{2,1,0:T(8,128)(2,1)}, u32[]{:S(2)}, u32[]{:S(2)}) async-start(bf16[4,256,512]{2,1,0:T(8,128)(2,1)} %broadcast_in_dim.56), calls=%async_computation.5 | async-start | bytes 2097152 | tf_op jit(solution)/shard_map/all_to_all | solution.py:11
  255.0 11.5 %collective-permute-start.1 = (bf16[256,512]{1,0:T(8,128)(2,1)}, bf16[256,512]{1,0:T(8,128)(2,1)}, u32[]{:S(2)}, u32[]{:S(2)}) collective-permute-start(bf16[256,512]{1,0:T(8,128)(2,1)} %get-tuple-element.23), channel_id=1, source_target_pairs={{64,0},{65,1},{66,2},{67,3},{68,4},{69,5},{70,6},{71,7},{72,8},{73... | collective-permute-start | bytes 786440 | tf_op jit(solution)/shard_map/ppermute | solution.py:51
  268.9 0.7 copy-start.11
  271.1 19.3 %all-to-all-start.5 = ((bf16[4,256,512]{2,1,0:T(8,128)(2,1)}), bf16[4,256,512]{2,1,0:T(8,128)(2,1)}, u32[]{:S(2)}, u32[]{:S(2)}) async-start(bf16[4,256,512]{2,1,0:T(8,128)(2,1)} %broadcast_in_dim.57), calls=%async_computation.6 | async-start | bytes 2097152 | tf_op jit(solution)/shard_map/all_to_all | solution.py:11
  293.6 10.3 %collective-permute-start.2 = (bf16[256,512]{1,0:T(8,128)(2,1)S(1)}, bf16[256,512]{1,0:T(8,128)(2,1)S(1)}, u32[]{:S(2)}, u32[]{:S(2)}) collective-permute-start(bf16[256,512]{1,0:T(8,128)(2,1)S(1)} %get-tuple-element.21), channel_id=1, source_target_pairs={{64,0},{65,1},{66,2},{67,3},{68,4},{69,5},{70,6},{71,7},{72,8},{73... | collective-permute-start | bytes 786440 | tf_op jit(solution)/shard_map/ppermute | solution.py:51
  303.9 0.7 copy-start.17
  306.2 0.7 copy-start.12
  308.4 19.6 %all-to-all-start.6 = ((bf16[4,256,512]{2,1,0:T(8,128)(2,1)}), bf16[4,256,512]{2,1,0:T(8,128)(2,1)}, u32[]{:S(2)}, u32[]{:S(2)}) async-start(bf16[4,256,512]{2,1,0:T(8,128)(2,1)} %broadcast_in_dim.58), calls=%async_computation.7 | async-start | bytes 2097152 | tf_op jit(solution)/shard_map/all_to_all | solution.py:11
  314.3 100.6 %reduce-scatter.7.cloned.1.call-start = ((), (), s32[]{:S(2)}) async-start(), calls=%async_computation.13 | async-start | bytes 1114112
  327.9 15.4 %copy-start.21 = (f32[256,512]{1,0:T(8,128)S(1)}, f32[256,512]{1,0:T(8,128)}, u32[]{:S(2)}) copy-start(f32[256,512]{1,0:T(8,128)} %fusion.21) | copy-start | bytes 1572868
  327.9 15.8 %copy-start.7 = (f32[512,512]{0,1:T(8,128)S(1)}, f32[512,512]{0,1:T(8,128)}, u32[]{:S(2)}) copy-start(f32[512,512]{0,1:T(8,128)} %fusion.4) | copy-start | bytes 3145732
  327.9 16.2 %copy-start.9 = (f32[512,512]{0,1:T(8,128)S(1)}, f32[512,512]{0,1:T(8,128)}, u32[]{:S(2)}) copy-start(f32[512,512]{0,1:T(8,128)} %fusion.2) | copy-start | bytes 3145732
  331.3 10.3 %collective-permute-start.3 = (bf16[256,512]{1,0:T(8,128)(2,1)S(1)}, bf16[256,512]{1,0:T(8,128)(2,1)S(1)}, u32[]{:S(2)}, u32[]{:S(2)}) collective-permute-start(bf16[256,512]{1,0:T(8,128)(2,1)S(1)} %get-tuple-element.19), channel_id=1, source_target_pairs={{64,0},{65,1},{66,2},{67,3},{68,4},{69,5},{70,6},{71,7},{72,8},{73... | collective-permute-start | bytes 786440 | tf_op jit(solution)/shard_map/ppermute | solution.py:51
  341.6 2.5 copy-start.15
  343.4 0.8 copy-start.18
  344.6 22.9 %copy-start.16 = (bf16[256,512]{1,0:T(8,128)(2,1)S(1)}, bf16[256,512]{1,0:T(8,128)(2,1)}, u32[]{:S(2)}) copy-start(bf16[256,512]{1,0:T(8,128)(2,1)} %copy-done.15) | copy-start | bytes 786436
  344.6 24.7 %copy-start.8 = (bf16[256,512]{1,0:T(8,128)(2,1)S(1)}, bf16[256,512]{1,0:T(8,128)(2,1)}, u32[]{:S(2)}) copy-start(bf16[256,512]{1,0:T(8,128)(2,1)} %param.7) | copy-start | bytes 786436
  348.5 18.9 %all-to-all-start.7 = ((bf16[4,256,512]{2,1,0:T(8,128)(2,1)}), bf16[4,256,512]{2,1,0:T(8,128)(2,1)S(1)}, u32[]{:S(2)}, u32[]{:S(2)}) async-start(bf16[4,256,512]{2,1,0:T(8,128)(2,1)} %broadcast_in_dim.59), calls=%async_computation.8 | async-start | bytes 2097152 | tf_op jit(solution)/shard_map/all_to_all | solution.py:11
  353.8 100.5 %all-gather.5.cloned.1.call-start = ((), (), s32[]{:S(2)}) async-start(), calls=%async_computation.12 | async-start | bytes 3145728 | tf_op jit(solution)/shard_map/all_gather | solution.py:55
Sparse Core Ops, SparseCore 0:
  10.7 54.5 all-gather.2
  228.2 76.3 reduce-scatter.4
  346.2 68.7 reduce-scatter.6
  416.4 37.8 all-gather.4
where the time goes:
time: 465 us; the launch traced here: 463 us
  waiting for transfers between devices  267 us (57%)
  other arithmetic  53.6 us (12%)
  matrix products  49 us (11%)
  starting transfers between devices  48.3 us (10%)
  local copies, waits for them, and re-layouts  30 us (6%)
  between operations  15.2 us (3%)
    all_to_all x8, waiting for transfers between devices, from_everyone(): return lax.all_to_all(copies, axis, split_axis=0, concat_axis=0, tiled=True)  111 us
    all_gather x1, waiting for transfers between devices, body(): columns = lax.all_gather(image_low, 'dp', axis=0, tiled=True)  52.9 us
    all_to_all x8, starting transfers between devices, from_everyone(): return lax.all_to_all(copies, axis, split_axis=0, concat_axis=0, tiled=True)  42.9 us
    unnamed x5, waiting for transfers between devices  42.6 us
    all_gather x1, waiting for transfers between devices, picked(): lax.all_gather(array, axis)  36.8 us
    dot_general x11, matrix products, contract_rows(): lax.dot_general(left_side, right_side, (((0,), (0,)), ((), ())), preferre...  25.3 us
    ppermute x4, waiting for transfers between devices, shifted(): return lax.ppermute(block, axis, route)  23.6 us
    dot_general x11, matrix products, contract_cols(): lax.dot_general(left_side, right_side, (((1,), (1,)), ((), ())), preferre...  16.1 us
  transfers between devices with their start and end apart: 16, of which 13 were waited for; matrix products, arithmetic and copies ran while one was open for 16% of the time, Pallas kernels for 0%

commit v1 on v0

--- a/solution.py
+++ b/solution.py
@@ -116,7 +116,21 @@
     image_unit, image_length = unit_rows(image_feats)
     text_low = text_unit.astype(jnp.bfloat16)
     image_low = image_unit.astype(jnp.bfloat16)
-    columns = lax.all_gather(image_low, "dp", axis=0, tiled=True)
+    ways, here, turn = (lax.axis_size("dp"), lax.axis_index("dp"), image_low.shape[0])
+    shape = [n * ways if d == 0 else n for d, n in enumerate(image_low.shape)]
+    full = lax.dynamic_update_slice_in_dim(
+        jnp.zeros(shape, image_low.dtype), image_low, here * turn, axis=0
+    )
+    going_up = going_down = image_low
+    for far in range(1, ways // 2 + 1):
+        going_up = lax.ppermute(going_up, "dp", [(d, (d + 1) % ways) for d in range(ways)])
+        full = lax.dynamic_update_slice_in_dim(full, going_up, (here - far) % ways * turn, axis=0)
+        if 2 * far < ways:
+            going_down = lax.ppermute(going_down, "dp", [(d, (d - 1) % ways) for d in range(ways)])
+            full = lax.dynamic_update_slice_in_dim(
+                full, going_down, (here + far) % ways * turn, axis=0
+            )
+    columns = full
     column_total_count = columns.shape[0]
     scores = logit_mult * contract_cols(text_low, columns)
     text_ids = dp_index * row_count + jnp.arange(row_count, dtype=jnp.int32)

time: 465 us -> 468 us (level)
  the two profiles are of different devices: /device:TPU:1 before, /device:TPU:0 now
where the time goes in v1:
time: 468 us; the launch traced here: 459 us
  waiting for transfers between devices  218 us (47%)
  starting transfers between devices  78.1 us (17%)
  other arithmetic  50.1 us (11%)
  local copies, waits for them, and re-layouts  47.5 us (10%)
  matrix products  47.3 us (10%)
  between operations  17.3 us (4%)
    all_to_all x8, waiting for transfers between devices, from_everyone(): return lax.all_to_all(copies, axis, split_axis=0, concat_axis=0, tiled=True)  117 us
    unnamed x4, waiting for transfers between devices  45.2 us
    ppermute x7, starting transfers between devices, body(): lax.ppermute(going_down, 'dp', [(d, (d - 1) % ways) for d in range(ways)])  37.9 us
    all_to_all x8, starting transfers between devices, from_everyone(): return lax.all_to_all(copies, axis, split_axis=0, concat_axis=0, tiled=True)  33 us
    ppermute x8, waiting for transfers between devices, body(): lax.ppermute(going_up, 'dp', [(d, (d + 1) % ways) for d in range(ways)])  29.3 us
    ppermute x4, waiting for transfers between devices, shifted(): return lax.ppermute(block, axis, route)  25.4 us
    dot_general x11, matrix products, contract_rows(): lax.dot_general(left_side, right_side, (((0,), (0,)), ((), ())), preferre...  24.3 us
    unnamed x62, local copies, waits for them, and re-layouts  16 us
  transfers between devices with their start and end apart: 30, of which 21 were waited for; matrix products, arithmetic and copies ran while one was open for 18% of the time, Pallas kernels for 0%

profile of v1, /device:TPU:0, one launch (start us, length us, event | category | flops | bytes accessed | tf_op | source)
XLA Modules:
  0.0 458.5 jit_solution(12900573784471223156)
XLA Ops:
  9.3 2.3 broadcast_in_dim.53
  12.4 1.7 collective-permute-start
  14.1 4.9 %collective-permute-start.1 = (bf16[256,512]{1,0:T(8,128)(2,1)S(1)}, bf16[256,512]{1,0:T(8,128)(2,1)S(1)}, u32[]{:S(2)}, u32[]{:S(2)}) collective-permute-start(bf16[256,512]{1,0:T(8,128)(2,1)S(1)} %get-tuple-element.39), channel_id=1, source_target_pairs={{0,60},{4,0},{8,4},{12,8},{16,12},{20,16},{24,20},{28,24},{32,28},... | collective-permute-start | bytes 786440 | tf_op jit(solution)/shard_map/ppermute | solution.py:129
  19.0 6.3 %collective-permute-done = bf16[256,512]{1,0:T(8,128)(2,1)S(1)} collective-permute-done((bf16[256,512]{1,0:T(8,128)(2,1)S(1)}, bf16[256,512]{1,0:T(8,128)(2,1)S(1)}, u32[]{:S(2)}, u32[]{:S(2)}) %collective-permute-start) | collective-permute-done | bytes 262176 | tf_op jit(solution)/shard_map/ppermute | solution.py:126
  25.3 5.3 %collective-permute-start.3 = (bf16[256,512]{1,0:T(8,128)(2,1)S(1)}, bf16[256,512]{1,0:T(8,128)(2,1)S(1)}, u32[]{:S(2)}, u32[]{:S(2)}) collective-permute-start(bf16[256,512]{1,0:T(8,128)(2,1)S(1)} %collective-permute-done.1), channel_id=1, source_target_pairs={{0,60},{4,0},{8,4},{12,8},{16,12},{20,16},{24,20},{28,24},{32,28},... | collective-permute-start | bytes 786440 | tf_op jit(solution)/shard_map/ppermute | solution.py:129
  30.9 5.2 %collective-permute-done.2 = bf16[256,512]{1,0:T(8,128)(2,1)S(1)} collective-permute-done((bf16[256,512]{1,0:T(8,128)(2,1)S(1)}, bf16[256,512]{1,0:T(8,128)(2,1)S(1)}, u32[]{:S(2)}, u32[]{:S(2)}) %collective-permute-start.2) | collective-permute-done | bytes 262176 | tf_op jit(solution)/shard_map/ppermute | solution.py:126
  36.1 5.4 %collective-permute-start.5 = (bf16[256,512]{1,0:T(8,128)(2,1)S(1)}, bf16[256,512]{1,0:T(8,128)(2,1)S(1)}, u32[]{:S(2)}, u32[]{:S(2)}) collective-permute-start(bf16[256,512]{1,0:T(8,128)(2,1)S(1)} %collective-permute-done.3), channel_id=1, source_target_pairs={{0,60},{4,0},{8,4},{12,8},{16,12},{20,16},{24,20},{28,24},{32,28},... | collective-permute-start | bytes 786440 | tf_op jit(solution)/shard_map/ppermute | solution.py:129
  41.5 4.6 %collective-permute-done.4 = bf16[256,512]{1,0:T(8,128)(2,1)} collective-permute-done((bf16[256,512]{1,0:T(8,128)(2,1)S(1)}, bf16[256,512]{1,0:T(8,128)(2,1)}, u32[]{:S(2)}, u32[]{:S(2)}) %collective-permute-start.4) | collective-permute-done | bytes 262176 | tf_op jit(solution)/shard_map/ppermute | solution.py:126
  46.8 1.7 constant_dynamic-update-slice_fusion.14
  48.5 5.3 %collective-permute-start.7 = (bf16[256,512]{1,0:T(8,128)(2,1)S(1)}, bf16[256,512]{1,0:T(8,128)(2,1)S(1)}, u32[]{:S(2)}, u32[]{:S(2)}) collective-permute-start(bf16[256,512]{1,0:T(8,128)(2,1)S(1)} %collective-permute-done.5), channel_id=1, source_target_pairs={{0,60},{4,0},{8,4},{12,8},{16,12},{20,16},{24,20},{28,24},{32,28},... | collective-permute-start | bytes 786440 | tf_op jit(solution)/shard_map/ppermute | solution.py:129
  54.6 1.6 collective-permute-done.6
  57.7 5.8 %collective-permute-start.9 = (bf16[256,512]{1,0:T(8,128)(2,1)S(1)}, bf16[256,512]{1,0:T(8,128)(2,1)S(1)}, u32[]{:S(2)}, u32[]{:S(2)}) collective-permute-start(bf16[256,512]{1,0:T(8,128)(2,1)S(1)} %collective-permute-done.7), channel_id=1, source_target_pairs={{0,60},{4,0},{8,4},{12,8},{16,12},{20,16},{24,20},{28,24},{32,28},... | collective-permute-start | bytes 786440 | tf_op jit(solution)/shard_map/ppermute | solution.py:129
  63.5 1.7 constant_dynamic-update-slice_fusion.10
  66.8 1.7 constant_dynamic-update-slice_fusion.8
  68.5 5.3 %collective-permute-start.11 = (bf16[256,512]{1,0:T(8,128)(2,1)S(1)}, bf16[256,512]{1,0:T(8,128)(2,1)S(1)}, u32[]{:S(2)}, u32[]{:S(2)}) collective-permute-start(bf16[256,512]{1,0:T(8,128)(2,1)S(1)} %collective-permute-done.9), channel_id=1, source_target_pairs={{0,60},{4,0},{8,4},{12,8},{16,12},{20,16},{24,20},{28,24},{32,28},... | collective-permute-start | bytes 786440 | tf_op jit(solution)/shard_map/ppermute | solution.py:129
  77.9 5.8 %collective-permute-start.13 = (bf16[256,512]{1,0:T(8,128)(2,1)S(1)}, bf16[256,512]{1,0:T(8,128)(2,1)S(1)}, u32[]{:S(2)}, u32[]{:S(2)}) collective-permute-start(bf16[256,512]{1,0:T(8,128)(2,1)S(1)} %collective-permute-done.11), channel_id=1, source_target_pairs={{0,60},{4,0},{8,4},{12,8},{16,12},{20,16},{24,20},{28,24},{32,28},... | collective-permute-start | bytes 786440 | tf_op jit(solution)/shard_map/ppermute | solution.py:129
  84.5 2.1 collective-permute-done.12
  88.7 7.5 %collective-permute-done.14 = bf16[256,512]{1,0:T(8,128)(2,1)S(1)} collective-permute-done((bf16[256,512]{1,0:T(8,128)(2,1)S(1)}, bf16[256,512]{1,0:T(8,128)(2,1)S(1)}, u32[]{:S(2)}, u32[]{:S(2)}) %collective-permute-start.14) | collective-permute-done | bytes 262176 | tf_op jit(solution)/shard_map/ppermute | solution.py:126
  97.0 6.6 %multiply_reduce_fusion.1 = (f32[1024]{0:T(1024)S(1)}, f32[1024,4096]{1,0:T(8,128)S(1)}) fusion(f32[]{:T(128)} %bitcast.111, bf16[4096,512]{1,0:T(8,128)(2,1)} %constant_dynamic-update-slice_fusion, f32[1024]{0:T(1024)S(1)} %add_sqrt_fusion, bf16[1024,512]{1,0:T(8,128)(2,1)S(1)} %copy-done.3), kind=kOutput, calls=%fused_computation.4 | convolution fusion | flops 4304927744 | bytes 22028292 | tf_op jit(solution)/shard_map/dot_general | solution.py:101
  103.6 4.3 exponential_reduce_fusion.1
  109.9 3.7 all-to-all-start
  113.7 8.5 %exponential_reduce_fusion = f32[4096]{0:T(1024)S(1)} fusion(f32[1024,4096]{1,0:T(8,128)} %copy-done.1, f32[4096]{0:T(1024)S(1)} %get-tuple-element.17, f32[]{:T(128)} %bitcast.115), kind=kLoop, calls=%fused_computation.1 | loop fusion | flops 12578816 | bytes 16809988 | tf_op jit(solution)/shard_map/reduce_sum | solution.py:145
  123.2 3.6 all-to-all-start.1
  127.1 12.2 %all-to-all-done.1 = f32[16,2,4096]{2,1,0:T(2,128)S(1)} async-done(((f32[16,2,4096]{2,1,0:T(2,128)}), f32[16,2,4096]{2,1,0:T(2,128)S(1)}, u32[]{:S(2)}, u32[]{:S(2)}) %all-to-all-start.1) | async-done | bytes 524320 | tf_op jit(solution)/shard_map/all_to_all | solution.py:11
  141.8 11.3 %subtract_convert_fusion = bf16[1024,4096]{1,0:T(8,128)(2,1)S(1)} fusion(f32[1024,4096]{1,0:T(8,128)} %copy-done.1, s32[4096]{0:T(1024)S(1)} %fusion.87, f32[4096]{0:T(1024)S(1)} %bitcast.117, f32[4096]{0:T(1024)S(1)} %bitcast.118, f32[1024]{0:T(1024)S(1)} %bitcast.120, f32[1024]{0:T(1024)S(1)} %bitcast.121, f32[]{:T(128)} %bitcast.114, s32[1024]{0:T(1024)S(1)} %iota_add_fusion), kind=kLoop, calls=%fused_computation | loop fusion | flops 46137344 | bytes 25227268 | tf_op jit(solution)/shard_map/convert_element_type | solution.py:149
  153.0 3.3 copy-done.4
  156.3 6.7 %multiply_convert_fusion.1 = bf16[1024,512]{1,0:T(8,128)(2,1)S(1)} fusion(bf16[1024,4096]{1,0:T(8,128)(2,1)S(1)} %subtract_convert_fusion, bf16[4096,512]{1,0:T(8,128)(2,1)} %constant_dynamic-update-slice_fusion, f32[]{:T(128)} %bitcast.112), kind=kOutput, calls=%fused_computation.17 | convolution fusion | flops 4296015872 | bytes 13631492 | tf_op jit(solution)/shard_map/dot_general | solution.py:150
  163.0 2.3 broadcast_in_dim.57
  165.2 5.1 %all-to-all-start.2 = ((bf16[4,1024,512]{2,1,0:T(8,128)(2,1)}), bf16[4,1024,512]{2,1,0:T(8,128)(2,1)}, u32[]{:S(2)}, u32[]{:S(2)}) async-start(bf16[4,1024,512]{2,1,0:T(8,128)(2,1)} %broadcast_in_dim.57), calls=%async_computation.3 | async-start | bytes 8388608 | tf_op jit(solution)/shard_map/all_to_all | solution.py:11
  170.7 47.8 %all-to-all-done.2 = bf16[4,1024,512]{2,1,0:T(8,128)(2,1)} async-done(((bf16[4,1024,512]{2,1,0:T(8,128)(2,1)}), bf16[4,1024,512]{2,1,0:T(8,128)(2,1)}, u32[]{:S(2)}, u32[]{:S(2)}) %all-to-all-start.2) | async-done | bytes 4194336 | tf_op jit(solution)/shard_map/all_to_all | solution.py:11
  218.6 3.1 convert_reduce_fusion
  226.2 4.3 all-to-all-start.3
  231.7 13.3 %all-to-all-done.3 = bf16[4,256,512]{2,1,0:T(8,128)(2,1)} async-done(((bf16[4,256,512]{2,1,0:T(8,128)(2,1)}), bf16[4,256,512]{2,1,0:T(8,128)(2,1)}, u32[]{:S(2)}, u32[]{:S(2)}) %all-to-all-start.3) | async-done | bytes 1048608 | tf_op jit(solution)/shard_map/all_to_all | solution.py:11
  245.0 1.4 convert_reduce_fusion.5
  247.5 1.7 select_dynamic-update-slice_fusion.3
  250.5 9.9 %multiply_convert_fusion = bf16[4096,512]{1,0:T(8,128)(2,1)} fusion(bf16[1024,4096]{1,0:T(8,128)(2,1)} %copy-done.4, f32[]{:T(128)} %bitcast.110, bf16[1024,512]{1,0:T(8,128)(2,1)S(1)} %copy-done.3, f32[1024]{0:T(1024)S(1)} %add_sqrt_fusion), kind=kOutput, calls=%fused_computation.6 | convolution fusion | flops 4300734464 | bytes 13635588 | tf_op jit(solution)/shard_map/dot_general | solution.py:95
  262.4 1.6 fusion.12
  265.4 4.2 all-to-all-start.4
  269.6 14.5 %all-to-all-done.4 = bf16[4,256,512]{2,1,0:T(8,128)(2,1)} async-done(((bf16[4,256,512]{2,1,0:T(8,128)(2,1)}), bf16[4,256,512]{2,1,0:T(8,128)(2,1)}, u32[]{:S(2)}, u32[]{:S(2)}) %all-to-all-start.4) | async-done | bytes 1048608 | tf_op jit(solution)/shard_map/all_to_all | solution.py:11
  284.1 1.4 convert_reduce_fusion.4
  285.6 1.9 select_dynamic-update-slice_fusion.2
  289.0 9.9 %collective-permute-done.16 = bf16[256,512]{1,0:T(8,128)(2,1)} collective-permute-done((bf16[256,512]{1,0:T(8,128)(2,1)S(1)}, bf16[256,512]{1,0:T(8,128)(2,1)}, u32[]{:S(2)}, u32[]{:S(2)}) %collective-permute-start.16) | collective-permute-done | bytes 262176 | tf_op jit(solution)/shard_map/ppermute | solution.py:51
  300.0 1.4 fusion.13
  303.5 4.3 all-to-all-start.5
  310.0 2.3 convolution_multiply_fusion.9
  312.3 2.4 convolution_multiply_fusion.4
  314.7 7.6 %all-to-all-done.5 = bf16[4,256,512]{2,1,0:T(8,128)(2,1)} async-done(((bf16[4,256,512]{2,1,0:T(8,128)(2,1)}), bf16[4,256,512]{2,1,0:T(8,128)(2,1)}, u32[]{:S(2)}, u32[]{:S(2)}) %all-to-all-start.5) | async-done | bytes 1048608 | tf_op jit(solution)/shard_map/all_to_all | solution.py:11
  322.3 1.5 convert_reduce_fusion.3
  323.8 1.8 select_dynamic-update-slice_fusion.1
  326.8 2.8 fusion.2
  329.7 7.0 %collective-permute-done.17 = bf16[256,512]{1,0:T(8,128)(2,1)S(1)} collective-permute-done((bf16[256,512]{1,0:T(8,128)(2,1)S(1)}, bf16[256,512]{1,0:T(8,128)(2,1)S(1)}, u32[]{:S(2)}, u32[]{:S(2)}) %collective-permute-start.17) | collective-permute-done | bytes 262176 | tf_op jit(solution)/shard_map/ppermute | solution.py:51
  340.0 4.2 all-to-all-start.6
  344.5 1.6 fusion.6
  348.9 9.9 %all-to-all-done.6 = bf16[4,256,512]{2,1,0:T(8,128)(2,1)} async-done(((bf16[4,256,512]{2,1,0:T(8,128)(2,1)}), bf16[4,256,512]{2,1,0:T(8,128)(2,1)}, u32[]{:S(2)}, u32[]{:S(2)}) %all-to-all-start.6) | async-done | bytes 1048608 | tf_op jit(solution)/shard_map/all_to_all | solution.py:11
  358.8 1.5 convert_reduce_fusion.2
  360.3 1.8 select_dynamic-update-slice_fusion
  363.3 1.4 convolution_multiply_fusion.1
  364.8 8.4 %collective-permute-done.18 = bf16[256,512]{1,0:T(8,128)(2,1)S(1)} collective-permute-done((bf16[256,512]{1,0:T(8,128)(2,1)S(1)}, bf16[256,512]{1,0:T(8,128)(2,1)S(1)}, u32[]{:S(2)}, u32[]{:S(2)}) %collective-permute-start.18) | collective-permute-done | bytes 262176 | tf_op jit(solution)/shard_map/ppermute | solution.py:51
  378.0 3.5 all-to-all-start.7
  381.6 2.3 copy.54
  383.9 12.0 %all-to-all-done.7 = bf16[4,256,512]{2,1,0:T(8,128)(2,1)S(1)} async-done(((bf16[4,256,512]{2,1,0:T(8,128)(2,1)}), bf16[4,256,512]{2,1,0:T(8,128)(2,1)S(1)}, u32[]{:S(2)}, u32[]{:S(2)}) %all-to-all-start.7) | async-done | bytes 1048608 | tf_op jit(solution)/shard_map/all_to_all | solution.py:11
  396.1 1.8 fusion.45
  399.1 1.9 fusion.19
  401.0 45.2 %reduce-scatter.7.cloned.1.call-done = bf16[32,1024]{1,0:T(8,128)(2,1)} async-done(((bf16[512,1024]{1,0:T(8,128)(2,1)}), bf16[32,1024]{1,0:T(8,128)(2,1)}) %reduce-scatter.7.cloned.1.call-update) | async-done | bytes 65552
  (177 shorter events, 57.6 us)
Async XLA Ops:
  8.0 162.4 %copy-start = (bf16[1,1024,512]{2,1,0:T(8,128)(2,1)S(1)}, bf16[1,1024,512]{2,1,0:T(8,128)(2,1)}, u32[]{:S(2)}) copy-start(bf16[1,1024,512]{2,1,0:T(8,128)(2,1)} %param.9) | copy-start | bytes 3145732
  8.0 3.5 copy-start.8
  8.0 22.6 %copy-start.3 = (bf16[1024,512]{1,0:T(8,128)(2,1)S(1)}, bf16[1024,512]{1,0:T(8,128)(2,1)}, u32[]{:S(2)}) copy-start(bf16[1024,512]{1,0:T(8,128)(2,1)} %param.6) | copy-start | bytes 3145732
  12.4 12.9 %collective-permute-start = (bf16[256,512]{1,0:T(8,128)(2,1)S(1)}, bf16[256,512]{1,0:T(8,128)(2,1)S(1)}, u32[]{:S(2)}, u32[]{:S(2)}) collective-permute-start(bf16[256,512]{1,0:T(8,128)(2,1)S(1)} %get-tuple-element.39), channel_id=1, source_target_pairs={{0,4},{4,8},{8,12},{12,16},{16,20},{20,24},{24,28},{28,32},{32,36}... | collective-permute-start | bytes 786440 | tf_op jit(solution)/shard_map/ppermute | solution.py:126
  14.1 11.2 %collective-permute-start.1 = (bf16[256,512]{1,0:T(8,128)(2,1)S(1)}, bf16[256,512]{1,0:T(8,128)(2,1)S(1)}, u32[]{:S(2)}, u32[]{:S(2)}) collective-permute-start(bf16[256,512]{1,0:T(8,128)(2,1)S(1)} %get-tuple-element.39), channel_id=1, source_target_pairs={{0,60},{4,0},{8,4},{12,8},{16,12},{20,16},{24,20},{28,24},{32,28},... | collective-permute-start | bytes 786440 | tf_op jit(solution)/shard_map/ppermute | solution.py:129
  25.3 10.8 %copy-start.24 = (bf16[256,512]{1,0:T(8,128)(2,1)}, bf16[256,512]{1,0:T(8,128)(2,1)S(1)}, u32[]{:S(2)}) copy-start(bf16[256,512]{1,0:T(8,128)(2,1)S(1)} %collective-permute-done) | copy-start | bytes 786436
  25.3 10.8 %collective-permute-start.2 = (bf16[256,512]{1,0:T(8,128)(2,1)S(1)}, bf16[256,512]{1,0:T(8,128)(2,1)S(1)}, u32[]{:S(2)}, u32[]{:S(2)}) collective-permute-start(bf16[256,512]{1,0:T(8,128)(2,1)S(1)} %collective-permute-done), channel_id=1, source_target_pairs={{0,4},{4,8},{8,12},{12,16},{16,20},{20,24},{24,28},{28,32},{32,36}... | collective-permute-start | bytes 786440 | tf_op jit(solution)/shard_map/ppermute | solution.py:126
  25.3 10.8 %collective-permute-start.3 = (bf16[256,512]{1,0:T(8,128)(2,1)S(1)}, bf16[256,512]{1,0:T(8,128)(2,1)S(1)}, u32[]{:S(2)}, u32[]{:S(2)}) collective-permute-start(bf16[256,512]{1,0:T(8,128)(2,1)S(1)} %collective-permute-done.1), channel_id=1, source_target_pairs={{0,60},{4,0},{8,4},{12,8},{16,12},{20,16},{24,20},{28,24},{32,28},... | collective-permute-start | bytes 786440 | tf_op jit(solution)/shard_map/ppermute | solution.py:129
  36.1 10.0 %collective-permute-start.4 = (bf16[256,512]{1,0:T(8,128)(2,1)S(1)}, bf16[256,512]{1,0:T(8,128)(2,1)}, u32[]{:S(2)}, u32[]{:S(2)}) collective-permute-start(bf16[256,512]{1,0:T(8,128)(2,1)S(1)} %collective-permute-done.2), channel_id=1, source_target_pairs={{0,4},{4,8},{8,12},{12,16},{16,20},{20,24},{24,28},{28,32},{32,36}... | collective-permute-start | bytes 786440 | tf_op jit(solution)/shard_map/ppermute | solution.py:126
  36.1 12.4 %collective-permute-start.5 = (bf16[256,512]{1,0:T(8,128)(2,1)S(1)}, bf16[256,512]{1,0:T(8,128)(2,1)S(1)}, u32[]{:S(2)}, u32[]{:S(2)}) collective-permute-start(bf16[256,512]{1,0:T(8,128)(2,1)S(1)} %collective-permute-done.3), channel_id=1, source_target_pairs={{0,60},{4,0},{8,4},{12,8},{16,12},{20,16},{24,20},{28,24},{32,28},... | collective-permute-start | bytes 786440 | tf_op jit(solution)/shard_map/ppermute | solution.py:129
  46.1 10.0 %collective-permute-start.6 = (bf16[256,512]{1,0:T(8,128)(2,1)}, bf16[256,512]{1,0:T(8,128)(2,1)}, u32[]{:S(2)}, u32[]{:S(2)}) collective-permute-start(bf16[256,512]{1,0:T(8,128)(2,1)} %collective-permute-done.4), channel_id=1, source_target_pairs={{0,4},{4,8},{8,12},{12,16},{16,20},{20,24},{24,28},{28,32},{32,36}... | collective-permute-start | bytes 786440 | tf_op jit(solution)/shard_map/ppermute | solution.py:126
  48.5 9.2 %collective-permute-start.7 = (bf16[256,512]{1,0:T(8,128)(2,1)S(1)}, bf16[256,512]{1,0:T(8,128)(2,1)S(1)}, u32[]{:S(2)}, u32[]{:S(2)}) collective-permute-start(bf16[256,512]{1,0:T(8,128)(2,1)S(1)} %collective-permute-done.5), channel_id=1, source_target_pairs={{0,60},{4,0},{8,4},{12,8},{16,12},{20,16},{24,20},{28,24},{32,28},... | collective-permute-start | bytes 786440 | tf_op jit(solution)/shard_map/ppermute | solution.py:129
  56.1 9.9 %collective-permute-start.8 = (bf16[256,512]{1,0:T(8,128)(2,1)}, bf16[256,512]{1,0:T(8,128)(2,1)S(1)}, u32[]{:S(2)}, u32[]{:S(2)}) collective-permute-start(bf16[256,512]{1,0:T(8,128)(2,1)} %collective-permute-done.6), channel_id=1, source_target_pairs={{0,4},{4,8},{8,12},{12,16},{16,20},{20,24},{24,28},{28,32},{32,36}... | collective-permute-start | bytes 786440 | tf_op jit(solution)/shard_map/ppermute | solution.py:126
  57.7 10.7 %collective-permute-start.9 = (bf16[256,512]{1,0:T(8,128)(2,1)S(1)}, bf16[256,512]{1,0:T(8,128)(2,1)S(1)}, u32[]{:S(2)}, u32[]{:S(2)}) collective-permute-start(bf16[256,512]{1,0:T(8,128)(2,1)S(1)} %collective-permute-done.7), channel_id=1, source_target_pairs={{0,60},{4,0},{8,4},{12,8},{16,12},{20,16},{24,20},{28,24},{32,28},... | collective-permute-start | bytes 786440 | tf_op jit(solution)/shard_map/ppermute | solution.py:129
  66.0 9.7 %collective-permute-start.10 = (bf16[256,512]{1,0:T(8,128)(2,1)S(1)}, bf16[256,512]{1,0:T(8,128)(2,1)S(1)}, u32[]{:S(2)}, u32[]{:S(2)}) collective-permute-start(bf16[256,512]{1,0:T(8,128)(2,1)S(1)} %collective-permute-done.8), channel_id=1, source_target_pairs={{0,4},{4,8},{8,12},{12,16},{16,20},{20,24},{24,28},{28,32},{32,36}... | collective-permute-start | bytes 786440 | tf_op jit(solution)/shard_map/ppermute | solution.py:126
  68.5 9.5 %collective-permute-start.11 = (bf16[256,512]{1,0:T(8,128)(2,1)S(1)}, bf16[256,512]{1,0:T(8,128)(2,1)S(1)}, u32[]{:S(2)}, u32[]{:S(2)}) collective-permute-start(bf16[256,512]{1,0:T(8,128)(2,1)S(1)} %collective-permute-done.9), channel_id=1, source_target_pairs={{0,60},{4,0},{8,4},{12,8},{16,12},{20,16},{24,20},{28,24},{32,28},... | collective-permute-start | bytes 786440 | tf_op jit(solution)/shard_map/ppermute | solution.py:129
  75.7 10.8 %collective-permute-start.12 = (bf16[256,512]{1,0:T(8,128)(2,1)S(1)}, bf16[256,512]{1,0:T(8,128)(2,1)S(1)}, u32[]{:S(2)}, u32[]{:S(2)}) collective-permute-start(bf16[256,512]{1,0:T(8,128)(2,1)S(1)} %collective-permute-done.10), channel_id=1, source_target_pairs={{0,4},{4,8},{8,12},{12,16},{16,20},{20,24},{24,28},{28,32},{32,36}... | collective-permute-start | bytes 786440 | tf_op jit(solution)/shard_map/ppermute | solution.py:126
  77.9 10.1 %collective-permute-start.13 = (bf16[256,512]{1,0:T(8,128)(2,1)S(1)}, bf16[256,512]{1,0:T(8,128)(2,1)S(1)}, u32[]{:S(2)}, u32[]{:S(2)}) collective-permute-start(bf16[256,512]{1,0:T(8,128)(2,1)S(1)} %collective-permute-done.11), channel_id=1, source_target_pairs={{0,60},{4,0},{8,4},{12,8},{16,12},{20,16},{24,20},{28,24},{32,28},... | collective-permute-start | bytes 786440 | tf_op jit(solution)/shard_map/ppermute | solution.py:129
  86.6 9.7 %collective-permute-start.14 = (bf16[256,512]{1,0:T(8,128)(2,1)S(1)}, bf16[256,512]{1,0:T(8,128)(2,1)S(1)}, u32[]{:S(2)}, u32[]{:S(2)}) collective-permute-start(bf16[256,512]{1,0:T(8,128)(2,1)S(1)} %collective-permute-done.12), channel_id=1, source_target_pairs={{0,4},{4,8},{8,12},{12,16},{16,20},{20,24},{24,28},{28,32},{32,36}... | collective-permute-start | bytes 786440 | tf_op jit(solution)/shard_map/ppermute | solution.py:126
  103.6 5.8 %copy-start.1 = (f32[1024,4096]{1,0:T(8,128)}, f32[1024,4096]{1,0:T(8,128)S(1)}, u32[]{:S(2)}) copy-start(f32[1024,4096]{1,0:T(8,128)S(1)} %get-tuple-element.47) | copy-start | bytes 50331652
  109.9 12.3 %all-to-all-start = ((f32[4,2,1024]{2,1,0:T(2,128)}), f32[4,2,1024]{2,1,0:T(2,128)S(1)}, u32[]{:S(2)}, u32[]{:S(2)}) async-start(f32[4,2,1024]{2,1,0:T(2,128)} %broadcast_in_dim.54), calls=%async_computation | async-start | bytes 65536 | tf_op jit(solution)/shard_map/all_to_all | solution.py:11
  123.2 16.0 %all-to-all-start.1 = ((f32[16,2,4096]{2,1,0:T(2,128)}), f32[16,2,4096]{2,1,0:T(2,128)S(1)}, u32[]{:S(2)}, u32[]{:S(2)}) async-start(f32[16,2,4096]{2,1,0:T(2,128)} %broadcast_in_dim.55), calls=%async_computation.1 | async-start | bytes 1048576 | tf_op jit(solution)/shard_map/all_to_all | solution.py:11
  153.0 3.3 copy-start.4
  165.2 5.2 %copy-start.2 = (bf16[1,512,512]{2,1,0:T(8,128)(2,1)S(1)}, bf16[1,512,512]{2,1,0:T(8,128)(2,1)}, u32[]{:S(2)}) copy-start(bf16[1,512,512]{2,1,0:T(8,128)(2,1)} %param.10) | copy-start | bytes 1572868
  165.2 53.3 %all-to-all-start.2 = ((bf16[4,1024,512]{2,1,0:T(8,128)(2,1)}), bf16[4,1024,512]{2,1,0:T(8,128)(2,1)}, u32[]{:S(2)}, u32[]{:S(2)}) async-start(bf16[4,1024,512]{2,1,0:T(8,128)(2,1)} %broadcast_in_dim.57), calls=%async_computation.3 | async-start | bytes 8388608 | tf_op jit(solution)/shard_map/all_to_all | solution.py:11
  170.7 52.0 %copy-start.21 = (f32[256,512]{1,0:T(8,128)}, f32[256,512]{1,0:T(8,128)S(1)}, u32[]{:S(2)}) copy-start(f32[256,512]{1,0:T(8,128)S(1)} %fusion.33) | copy-start | bytes 1572868
  221.7 2.0 copy-start.25
  222.7 1.0 copy-start.5
  224.1 0.7 copy-start.15
  226.2 18.8 %all-to-all-start.3 = ((bf16[4,256,512]{2,1,0:T(8,128)(2,1)}), bf16[4,256,512]{2,1,0:T(8,128)(2,1)}, u32[]{:S(2)}, u32[]{:S(2)}) async-start(bf16[4,256,512]{2,1,0:T(8,128)(2,1)} %broadcast_in_dim.59), calls=%async_computation.4 | async-start | bytes 2097152 | tf_op jit(solution)/shard_map/all_to_all | solution.py:11
  230.5 167.4 %reduce-scatter.5.cloned.1.call-start = ((), (), s32[]{:S(2)}) async-start(), calls=%async_computation.10 | async-start | bytes 4456448 | tf_op jit(solution)/shard_map/reduce_scatter | solution.py:153
  249.2 11.2 %collective-permute-start.15 = (bf16[256,512]{1,0:T(8,128)(2,1)S(1)}, bf16[256,512]{1,0:T(8,128)(2,1)S(1)}, u32[]{:S(2)}, u32[]{:S(2)}) collective-permute-start(bf16[256,512]{1,0:T(8,128)(2,1)S(1)} %get-tuple-element.25), channel_id=1, source_target_pairs={{64,0},{65,1},{66,2},{67,3},{68,4},{69,5},{70,6},{71,7},{72,8},{73... | collective-permute-start | bytes 786440 | tf_op jit(solution)/shard_map/ppermute | solution.py:51
  260.4 1.2 copy-start.6
  261.7 0.7 copy-start.16
  265.4 18.7 %all-to-all-start.4 = ((bf16[4,256,512]{2,1,0:T(8,128)(2,1)}), bf16[4,256,512]{2,1,0:T(8,128)(2,1)}, u32[]{:S(2)}, u32[]{:S(2)}) async-start(bf16[4,256,512]{2,1,0:T(8,128)(2,1)} %broadcast_in_dim.60), calls=%async_computation.5 | async-start | bytes 2097152 | tf_op jit(solution)/shard_map/all_to_all | solution.py:11
  287.4 11.6 %collective-permute-start.16 = (bf16[256,512]{1,0:T(8,128)(2,1)S(1)}, bf16[256,512]{1,0:T(8,128)(2,1)}, u32[]{:S(2)}, u32[]{:S(2)}) collective-permute-start(bf16[256,512]{1,0:T(8,128)(2,1)S(1)} %get-tuple-element.23), channel_id=1, source_target_pairs={{64,0},{65,1},{66,2},{67,3},{68,4},{69,5},{70,6},{71,7},{72,8},{73... | collective-permute-start | bytes 786440 | tf_op jit(solution)/shard_map/ppermute | solution.py:51
  289.0 10.9 %copy-start.9 = (f32[256,512]{1,0:T(8,128)}, f32[256,512]{1,0:T(8,128)S(1)}, u32[]{:S(2)}) copy-start(f32[256,512]{1,0:T(8,128)S(1)} %fusion.27) | copy-start | bytes 1572868
  301.4 0.7 copy-start.12
  303.5 18.8 %all-to-all-start.5 = ((bf16[4,256,512]{2,1,0:T(8,128)(2,1)}), bf16[4,256,512]{2,1,0:T(8,128)(2,1)}, u32[]{:S(2)}, u32[]{:S(2)}) async-start(bf16[4,256,512]{2,1,0:T(8,128)(2,1)} %broadcast_in_dim.61), calls=%async_computation.6 | async-start | bytes 2097152 | tf_op jit(solution)/shard_map/all_to_all | solution.py:11
  322.3 15.2 %copy-start.22 = (f32[256,512]{1,0:T(8,128)S(1)}, f32[256,512]{1,0:T(8,128)}, u32[]{:S(2)}) copy-start(f32[256,512]{1,0:T(8,128)} %fusion.24) | copy-start | bytes 1572868
  322.3 15.2 %copy-start.26 = (bf16[1,512,512]{2,1,0:T(8,128)(2,1)S(1)}, bf16[1,512,512]{2,1,0:T(8,128)(2,1)}, u32[]{:S(2)}) copy-start(bf16[1,512,512]{2,1,0:T(8,128)(2,1)} %param.11) | copy-start | bytes 1572868
  325.6 11.2 %collective-permute-start.17 = (bf16[256,512]{1,0:T(8,128)(2,1)S(1)}, bf16[256,512]{1,0:T(8,128)(2,1)S(1)}, u32[]{:S(2)}, u32[]{:S(2)}) collective-permute-start(bf16[256,512]{1,0:T(8,128)(2,1)S(1)} %get-tuple-element.21), channel_id=1, source_target_pairs={{64,0},{65,1},{66,2},{67,3},{68,4},{69,5},{70,6},{71,7},{72,8},{73... | collective-permute-start | bytes 786440 | tf_op jit(solution)/shard_map/ppermute | solution.py:51
  336.8 0.7 copy-start.17
  337.9 0.7 copy-start.13
  340.0 18.7 %all-to-all-start.6 = ((bf16[4,256,512]{2,1,0:T(8,128)(2,1)}), bf16[4,256,512]{2,1,0:T(8,128)(2,1)}, u32[]{:S(2)}, u32[]{:S(2)}) async-start(bf16[4,256,512]{2,1,0:T(8,128)(2,1)} %broadcast_in_dim.62), calls=%async_computation.7 | async-start | bytes 2097152 | tf_op jit(solution)/shard_map/all_to_all | solution.py:11
  344.3 101.9 %reduce-scatter.7.cloned.1.call-start = ((), (), s32[]{:S(2)}) async-start(), calls=%async_computation.12 | async-start | bytes 1114112
  344.5 3.0 copy-start.14
  346.1 14.1 %copy-start.18 = (bf16[256,512]{1,0:T(8,128)(2,1)S(1)}, bf16[256,512]{1,0:T(8,128)(2,1)}, u32[]{:S(2)}) copy-start(bf16[256,512]{1,0:T(8,128)(2,1)} %copy-done.17) | copy-start | bytes 786436
  358.8 14.5 %copy-start.23 = (f32[256,512]{1,0:T(8,128)S(1)}, f32[256,512]{1,0:T(8,128)}, u32[]{:S(2)}) copy-start(f32[256,512]{1,0:T(8,128)} %fusion.21) | copy-start | bytes 1572868
  358.8 14.5 %copy-start.27 = (bf16[1,512,512]{2,1,0:T(8,128)(2,1)S(1)}, bf16[1,512,512]{2,1,0:T(8,128)(2,1)}, u32[]{:S(2)}) copy-start(bf16[1,512,512]{2,1,0:T(8,128)(2,1)} %param.11) | copy-start | bytes 1572868
  362.1 11.1 %collective-permute-start.18 = (bf16[256,512]{1,0:T(8,128)(2,1)S(1)}, bf16[256,512]{1,0:T(8,128)(2,1)S(1)}, u32[]{:S(2)}, u32[]{:S(2)}) collective-permute-start(bf16[256,512]{1,0:T(8,128)(2,1)S(1)} %get-tuple-element.19), channel_id=1, source_target_pairs={{64,0},{65,1},{66,2},{67,3},{68,4},{69,5},{70,6},{71,7},{72,8},{73... | collective-permute-start | bytes 786440 | tf_op jit(solution)/shard_map/ppermute | solution.py:51
  364.8 9.3 %copy-start.7 = (f32[512,512]{0,1:T(8,128)S(1)}, f32[512,512]{0,1:T(8,128)}, u32[]{:S(2)}) copy-start(f32[512,512]{0,1:T(8,128)} %fusion.4) | copy-start | bytes 3145732
  373.2 1.2 copy-start.10
  373.3 1.5 copy-start.11
  373.7 0.8 copy-start.19
  375.2 1.4 copy-start.20
  378.0 17.9 %all-to-all-start.7 = ((bf16[4,256,512]{2,1,0:T(8,128)(2,1)}), bf16[4,256,512]{2,1,0:T(8,128)(2,1)S(1)}, u32[]{:S(2)}, u32[]{:S(2)}) async-start(bf16[4,256,512]{2,1,0:T(8,128)(2,1)} %broadcast_in_dim.63), calls=%async_computation.8 | async-start | bytes 2097152 | tf_op jit(solution)/shard_map/all_to_all | solution.py:11
  381.6 67.2 %all-gather.2.cloned.1.call-start = ((), (), s32[]{:S(2)}) async-start(), calls=%async_computation.11 | async-start | bytes 3145728 | tf_op jit(solution)/shard_map/all_gather | solution.py:55
Sparse Core Ops, SparseCore 0:
  260.6 77.3 reduce-scatter.4
  376.7 69.3 reduce-scatter.6
Sparse Core Ops, SparseCore 1:
  398.0 32.0 all-gather.1
